TPU v7x, 32 devices: a whole 2x2x4 slice. The times are simulated.
32 devices in a mesh: dp: 8 (over z, y), tensor: 4 (over x, core).
Axes of the slice: x: 2, y: 2, z: 4, core: 2. Of those that a mesh axis runs over, the one named last changes fastest.
Arguments:
- tokens: bfloat16 [8704, 1024], P(('dp', 'tensor')), may hold values from -6 to 6
- text_lengths: int32 [8], P('dp'), may hold values from 1 to 64, as said below
- norm1_gain: float32 [1024], replicated, may hold values from 0.25 to 1.75
- norm1_shift: float32 [1024], replicated, may hold values from -1.75 to 1.75
- w_qkv: bfloat16 [1024, 3072], P(None, 'tensor'), may hold values from -0.25 to 0.25
- q_bias: float32 [1024], P('tensor'), may hold values from -1.75 to 1.75
- v_bias: float32 [1024], P('tensor'), may hold values from -1.75 to 1.75
- w_out: bfloat16 [1024, 1024], P('tensor'), may hold values from -1 to 1
- out_bias: float32 [1024], replicated, may hold values from -1.75 to 1.75
- norm2_gain: float32 [1024], replicated, may hold values from 0.25 to 1.75
- norm2_shift: float32 [1024], replicated, may hold values from -1.75 to 1.75
- norm3_gain: float32 [1024], replicated, may hold values from 0.25 to 1.75
- norm3_shift: float32 [1024], replicated, may hold values from -1.75 to 1.75
- w_fc1: bfloat16 [1024, 4096], P(None, 'tensor'), may hold values from -0.1875 to 0.1875
- fc1_bias: bfloat16 [4096], P('tensor'), may hold values from -3 to 3
- w_fc2: bfloat16 [4096, 1024], P('tensor'), may hold values from -0.09375 to 0.09375
- fc2_bias: float32 [1024], replicated, may hold values from -1.75 to 1.75
- norm4_gain: float32 [1024], replicated, may hold values from 0.25 to 1.75
- norm4_shift: float32 [1024], replicated, may hold values from -1.75 to 1.75
- cotangent: bfloat16 [8704, 1024], P(('dp', 'tensor')), may hold values from -16 to 16
Outputs:
- layer_out: bfloat16 [8704, 1024], P(('dp', 'tensor'))
- input_grad: float32 [8704, 1024], P(('dp', 'tensor'))
- grad_norm1_gain: float32 [1024], replicated
- grad_norm1_shift: float32 [1024], replicated
- grad_qkv: float32 [1024, 3072], P(None, 'tensor')
- grad_q_bias: float32 [1024], P('tensor')
- grad_v_bias: float32 [1024], P('tensor')
- grad_out: float32 [1024, 1024], P('tensor')
- grad_out_bias: float32 [1024], replicated
- grad_norm2_gain: float32 [1024], replicated
- grad_norm2_shift: float32 [1024], replicated
- grad_norm3_gain: float32 [1024], replicated
- grad_norm3_shift: float32 [1024], replicated
- grad_fc1: float32 [1024, 4096], P(None, 'tensor')
- grad_fc1_bias: float32 [4096], P('tensor')
- grad_fc2: float32 [4096, 1024], P('tensor')
- grad_fc2_bias: float32 [1024], replicated
- grad_norm4_gain: float32 [1024], replicated
- grad_norm4_shift: float32 [1024], replicated
Inputs may be any that keep to these rules, and one draw needn't show every extreme that they name: `text_lengths`: some sequence has all 64 text positions real and some has only one.
All inputs are finite; a program needn't handle non-finite values.
Results may differ from a plain program's by a relative error of at most 0.014.
The roundings to bfloat16 on the way count: a program that leaves them out, or rounds other values in their place, can miss the bound.
Values may be sent and summed in bfloat16 or wider, within the bound.
A program may use at most 192 MiB of HBM per device.

v0:
```python
from functools import partial
import math

import jax
import jax.numpy as jnp
from jax import lax
from jax.experimental import pallas as pl
from jax.experimental.pallas import tpu as pltpu
from jax.sharding import PartitionSpec as P

HD = 64
TEXT = 64


epsilon = 1e-05


def times_transposed(left, right):
    return lax.dot_general(
        left, right, (((1,), (1,)), ((), ())), preferred_element_type=jnp.float32
    )


def transposed_times(left, right):
    return lax.dot_general(
        left, right, (((0,), (0,)), ((), ())), preferred_element_type=jnp.float32
    )


STEP = 64
TILE = 256
MESH = pl.DeviceIdType.MESH
LOW = jnp.bfloat16


def statistics(values):
    centered = values - jnp.mean(values, axis=-1, keepdims=True)
    inverse = lax.rsqrt(jnp.mean(centered * centered, axis=-1, keepdims=True) + epsilon)
    return centered * inverse, inverse


def norm_pullback(grad, normed, inverse, gain):
    scaled = grad * gain
    return inverse * (
        scaled
        - jnp.mean(scaled, axis=-1, keepdims=True)
        - normed * jnp.mean(scaled * normed, axis=-1, keepdims=True)
    )


def before_attention(total, rows, vectors):
    (token_rows,), (gain, shift) = rows, vectors
    normed, _ = statistics(token_rows)
    return normed * gain + shift, (), ()


def after_attention(total, rows, vectors):
    (token_rows,), (bias, gain2, shift2, gain3, shift3) = rows, vectors
    branch = total + bias
    normed, _ = statistics(branch)
    hidden = token_rows + (normed * gain2 + shift2)
    third, _ = statistics(hidden)
    return third * gain3 + shift3, (branch, hidden), ()


def turn_round(total, rows, vectors):
    (hidden, grad), (bias, gain, shift) = rows, vectors
    normed, inverse = statistics(total + bias)
    layer_out = hidden + (normed * gain + shift)
    low = norm_pullback(grad, normed, inverse, gain).astype(LOW).astype(jnp.float32)
    return low, (layer_out,), (grad * normed, grad, low)


def after_feed_forward(total, rows, vectors):
    (branch, hidden, grad), (gain2, gain3) = rows, vectors
    third, inverse3 = statistics(hidden)
    grad_hidden = grad + norm_pullback(total, third, inverse3, gain3)
    second, inverse2 = statistics(branch)
    low = norm_pullback(grad_hidden, second, inverse2, gain2).astype(LOW).astype(jnp.float32)
    return low, (grad_hidden,), (total * third, total, grad_hidden * second, grad_hidden, low)


def at_the_input(total, rows, vectors):
    (token_rows, grad_hidden), (gain,) = rows, vectors
    first, inverse = statistics(token_rows)
    return None, (grad_hidden + norm_pullback(total, first, inverse, gain),), (total * first, total)


class GroupSum:
    def __init__(self, sources, results, scratch):
        self.kept, self.near, self.far = scratch[:3]
        self.sems = scratch[3:]
        self.sources, self.results = sources, results
        self.pieces = [
            (at, column)
            for at, source in enumerate(sources)
            for column in range(0, source.shape[1], TILE)
        ]
        self.half = sources[0].shape[0] // 2
        self.peers = lax.axis_size("dp") // 2
        self.part = self.half // self.peers
        group = lax.axis_index("dp")
        self.side = lax.rem(group, 2)
        self.place = lax.div(group, 2)
        self.partner = group + 1 - 2 * self.side

    def others(self):
        for hop in range(1, self.peers):
            yield (
                hop - 1,
                lax.rem(self.place + hop, self.peers),
                lax.rem(self.place + self.peers - hop, self.peers),
            )

    def device(self, place):
        return place * 2 + self.side

    def targets(self):
        return [self.partner] + [self.device(ahead) for _, ahead, _ in self.others()]

    def send(self, source, target, outgoing, incoming, device):
        return pltpu.make_async_remote_copy(
            source, target, outgoing, incoming,
            device_id={"dp": device}, device_id_type=MESH,
        )

    def rows(self, start, size):
        return pl.ds(pl.multiple_of(start, 16), size)

    def cuts(self, piece):
        at, column = self.pieces[piece]
        return self.sources[at], self.results[at], pl.ds(column, TILE), pl.ds(piece * TILE, TILE)

    def halving(self, piece):
        source, _, cut, held = self.cuts(piece)
        return self.send(
            source.at[self.rows((1 - self.side) * self.half, self.half), cut],
            self.near.at[:, held], self.sems[0].at[piece], self.sems[1].at[piece], self.partner,
        )

    def parting(self, piece, slot, ahead):
        held = pl.ds(piece * TILE, TILE)
        return self.send(
            self.kept.at[self.rows(ahead * self.part, self.part), held], self.far.at[slot, :, held],
            self.sems[2].at[slot, piece], self.sems[3].at[slot, piece], self.device(ahead),
        )

    def joining(self, piece, slot, owner, ahead):
        _, result, cut, _ = self.cuts(piece)
        region = result.at[self.rows(self.side * self.half + owner * self.part, self.part), cut]
        return self.send(
            region, region, self.sems[4].at[slot, piece], self.sems[5].at[slot, piece],
            self.device(ahead),
        )

    def doubling(self, piece, side):
        _, result, cut, _ = self.cuts(piece)
        region = result.at[self.rows(side * self.half, self.half), cut]
        return self.send(
            region, region, self.sems[6].at[piece], self.sems[7].at[piece], self.partner
        )

    def start(self):
        for piece in range(len(self.pieces)):
            self.halving(piece).start()

    def after_halving(self, piece):
        source, _, cut, held = self.cuts(piece)
        self.halving(piece).wait_recv()
        mine = source[self.rows(self.side * self.half, self.half), cut].astype(jnp.float32)
        self.kept[:, held] = (mine + self.near[:, held].astype(jnp.float32)).astype(LOW)
        for slot, ahead, _ in self.others():
            self.parting(piece, slot, ahead).start()

    def after_parting(self, piece):
        _, result, cut, held = self.cuts(piece)
        total = self.kept[self.rows(self.place * self.part, self.part), held].astype(jnp.float32)
        for slot, ahead, _ in self.others():
            self.parting(piece, slot, ahead).wait_recv()
            total = total + self.far[slot, :, held].astype(jnp.float32)
        own = self.rows(self.side * self.half + self.place * self.part, self.part)
        result[own, cut] = total.astype(LOW)
        for slot, ahead, _ in self.others():
            self.joining(piece, slot, self.place, ahead).start()

    def after_joining(self, piece):
        for slot, ahead, behind in self.others():
            self.joining(piece, slot, behind, ahead).wait_recv()
        self.doubling(piece, self.side).start()

    def settle(self, piece):
        self.doubling(piece, 1 - self.side).wait_recv()
        self.doubling(piece, self.side).wait_send()
        self.halving(piece).wait_send()
        for slot, ahead, _ in self.others():
            self.parting(piece, slot, ahead).wait_send()
            self.joining(piece, slot, self.place, ahead).wait_send()


def group_sum_scratch(sources):
    pieces = sum(source.shape[1] for source in sources) // TILE
    half = sources[0].shape[0] // 2
    peers = lax.axis_size("dp") // 2
    width = pieces * TILE
    pair, fan = pltpu.SemaphoreType.DMA((pieces,)), pltpu.SemaphoreType.DMA((peers - 1, pieces))
    return [
        pltpu.VMEM((half, width), LOW),
        pltpu.VMEM((half, width), LOW),
        pltpu.VMEM((peers - 1, half // peers, width), LOW),
    ] + [pair, pair, fan, fan, fan, fan, pair, pair]


class SmallSum:
    def __init__(self, shared, owned, fresh, shared_out, owned_out, part, parts, turn, turns, last,
                 lasts, part_out, part_in, turn_out, turn_in, last_out, last_in):
        self.shared, self.owned, self.fresh = shared, owned, fresh
        self.shared_out, self.owned_out = shared_out, owned_out
        self.part, self.parts, self.turn, self.turns = part, parts, turn, turns
        self.last, self.lasts = last, lasts
        self.sems = part_out, part_in, turn_out, turn_in, last_out, last_in
        self.places, groups = lax.axis_size("tensor"), lax.axis_size("dp")
        self.groups = groups
        self.me, self.group = lax.axis_index("tensor"), lax.axis_index("dp")
        self.peers = [lax.rem(self.me + hop, self.places) for hop in range(1, self.places)]
        self.others = [lax.rem(self.group + hop, groups) for hop in range(1, groups)]
        self.n_fresh = fresh.shape[0]
        self.n_shared = self.n_fresh + shared.shape[0]
        self.quarter = shared.shape[-1] // self.places

    def sends(self, stage):
        axis = "dp" if stage == 1 else "tensor"
        outgoing, incoming = self.sems[2 * stage], self.sems[2 * stage + 1]
        for hop, peer in enumerate(self.others if stage == 1 else self.peers):
            if stage == 0:
                source, target = self.part.at[peer], self.parts.at[hop]
            elif stage == 1:
                source, target = self.turn, self.turns.at[self.group]
            else:
                source, target = self.last, self.lasts.at[self.me]
            yield pltpu.make_async_remote_copy(
                source, target, outgoing.at[hop], incoming.at[hop],
                device_id={axis: peer}, device_id_type=MESH,
            )

    def first_send(self):
        for place in range(self.places):
            cut = slice(place * self.quarter, (place + 1) * self.quarter)
            self.part[place, : self.n_fresh] = jnp.sum(self.fresh[:, :, cut], axis=1)
            self.part[place, self.n_fresh :] = jnp.sum(self.shared[:, :, cut], axis=1)
        for send in self.sends(0):
            send.start()

    def first_wait(self):
        total = self.part[self.me]
        for hop, send in enumerate(self.sends(0)):
            send.wait()
            total = total + self.parts[hop]
        self.turn[: self.n_shared] = total
        self.turn[self.n_shared :] = self.owned[...]
        self.turns[self.group] = self.turn[...]

    def second_send(self):
        for send in self.sends(1):
            send.start()

    def second_wait(self):
        for send in self.sends(1):
            send.wait()
        total = self.turns[0]
        for at in range(1, self.groups):
            total = total + self.turns[at]
        self.owned_out[...] = total[self.n_shared :]
        self.last[...] = total[: self.n_shared]
        self.lasts[self.me] = total[: self.n_shared]

    def third_send(self):
        for send in self.sends(2):
            send.start()

    def third_wait(self):
        for send in self.sends(2):
            send.wait()
        for place in range(self.places):
            cut = slice(place * self.quarter, (place + 1) * self.quarter)
            self.shared_out[:, cut] = self.lasts[place]


def small_sum_scratch(n_shared, owned):
    places, groups = lax.axis_size("tensor"), lax.axis_size("dp")
    quarter = owned.shape[1]
    depth = n_shared + owned.shape[0]
    return [
        pltpu.VMEM((places, n_shared, quarter), jnp.float32),
        pltpu.VMEM((places - 1, n_shared, quarter), jnp.float32),
        pltpu.VMEM((depth, quarter), jnp.float32),
        pltpu.VMEM((groups, depth, quarter), jnp.float32),
        pltpu.VMEM((n_shared, quarter), jnp.float32),
        pltpu.VMEM((places, n_shared, quarter), jnp.float32),
    ] + [
        pltpu.SemaphoreType.DMA((count,))
        for count in (places - 1, places - 1, groups - 1, groups - 1, places - 1, places - 1)
    ]


def segment_kernel(middle, counts, flipped, sending, *refs):
    n_rows, n_vectors, n_outs, n_sums, n_grouped = counts
    refs = list(refs)

    def take(count):
        taken = refs[:count]
        del refs[:count]
        return taken

    summing = flipped is not None
    if summing:
        left, right = take(2)
    row_refs, vector_refs = take(n_rows), take(n_vectors)
    if n_grouped:
        group_sources = take(n_grouped)
        small_in = take(2)
    gathered = take(1)[0] if sending else None
    out_refs = take(n_outs)
    if n_grouped:
        group_results = take(n_grouped)
        small_out = take(2)
    sums = take(1)[0] if n_sums else None
    if summing:
        give, got, keep, onward, came, give_sem, got_sem, out_sem, in_sem = take(9)
    if sending:
        near_out, near_in, far_out, far_in, on_out, on_in = take(6)
    if n_grouped:
        grouped = GroupSum(group_sources, group_results, take(11))
        small = SmallSum(*small_in, sums, *small_out, *take(12))

    me = lax.axis_index("tensor")
    partner = me + 1 - 2 * lax.rem(me, 2)
    across = lax.rem(me + 2, 4)
    diagonal = 3 - me
    share, width = row_refs[0].shape
    whole = share // STEP
    rest = share - whole * STEP

    def each(body):
        def one(at, carry):
            body(at, pl.multiple_of(at * STEP, STEP), STEP)
            return carry

        lax.fori_loop(0, whole, one, 0)
        if rest:
            body(whole, whole * STEP, rest)

    barrier = pltpu.get_barrier_semaphore()
    for peer in (partner, across):
        pl.semaphore_signal(barrier, inc=1, device_id={"tensor": peer}, device_id_type=MESH)
    if n_grouped:
        pl.semaphore_signal(
            barrier, inc=1, device_id={"tensor": diagonal}, device_id_type=MESH
        )
        for other in small.others:
            pl.semaphore_signal(barrier, inc=1, device_id={"dp": other}, device_id_type=MESH)
        pl.semaphore_wait(barrier, 3 + len(small.others))
        grouped.start()
    else:
        pl.semaphore_wait(barrier, 2)

    def product(block, target):
        rows = pl.ds(pl.multiple_of(block * share, 16), share)

        def one(at, carry):
            cut = pl.ds(pl.multiple_of(at * TILE, TILE), TILE)
            if flipped:
                value = times_transposed(left[rows, :], right[cut, :])
            else:
                value = jnp.dot(left[rows, :], right[:, cut], preferred_element_type=jnp.float32)
            target[:, cut] = value.astype(target.dtype)
            return carry

        lax.fori_loop(0, width // TILE, one, 0)

    if summing:

        def gift(at):
            return pltpu.make_async_remote_copy(
                give.at[at], got.at[at], give_sem.at[at], got_sem.at[at],
                device_id={"tensor": partner}, device_id_type=MESH,
            )

        def crossing(at, start, size):
            cut = pl.ds(start, size)
            return pltpu.make_async_remote_copy(
                onward.at[cut], came.at[cut], out_sem.at[at], in_sem.at[at],
                device_id={"tensor": across}, device_id_type=MESH,
            )

        product(diagonal, give.at[0])
        product(across, keep.at[0])
        gift(0).start()
        product(partner, give.at[1])
        gift(0).wait_recv()

        def pass_on(at, start, size):
            cut = pl.ds(start, size)
            onward[cut] = (keep[0, cut] + got[0, cut].astype(jnp.float32)).astype(LOW)
            crossing(at, start, size).start()

        each(pass_on)
        gift(1).start()
        product(me, keep.at[1])
        gift(1).wait_recv()

    if n_sums:
        sums[...] = jnp.zeros_like(sums)
    vectors = [ref[...] for ref in vector_refs]

    def spread(target, block, sems, at, start, size):
        cut = pl.ds(pl.multiple_of(block * share + start, 16), size)
        return pltpu.make_async_remote_copy(
            gathered.at[cut], gathered.at[cut], sems[0].at[at], sems[1].at[at],
            device_id={"tensor": target}, device_id_type=MESH,
        )

    def finish(at, start, size):
        cut = pl.ds(start, size)
        total = None
        if summing:
            crossing(at, start, size).wait_recv()
            total = (
                keep[1, cut] + got[1, cut].astype(jnp.float32) + came[cut].astype(jnp.float32)
            )
        result, outs, terms = middle(
            total, [ref[cut].astype(jnp.float32) for ref in row_refs], vectors
        )
        if sending:
            own = pl.ds(pl.multiple_of(me * share + start, 16), size)
            gathered[own] = result.astype(LOW)
        for ref, value in zip(out_refs, outs):
            ref[cut] = value.astype(ref.dtype)
        for index, term in enumerate(terms):
            sums[index] += jnp.sum(term.reshape(size // 8, 8, width), axis=0)
        if sending:
            spread(across, me, (far_out, far_in), at, start, size).start()
            spread(partner, me, (near_out, near_in), at, start, size).start()

    if n_grouped:
        pieces = len(grouped.pieces)
        early = pieces // 2
        for piece in range(early):
            grouped.after_halving(piece)
        each(finish)
        small.first_send()
        for piece in range(early, pieces):
            grouped.after_halving(piece)
            grouped.after_parting(piece - early)
        small.first_wait()
        small.second_send()
        for piece in range(pieces - early, pieces):
            grouped.after_joining(piece - (pieces - early))
            grouped.after_parting(piece)
        small.second_wait()
        small.third_send()
        for piece in range(early, pieces):
            grouped.after_joining(piece)
        small.third_wait()
        for piece in range(pieces):
            grouped.settle(piece)
    else:
        each(finish)

    if sending:

        def relay(at, start, size):
            spread(across, across, (far_out, far_in), at, start, size).wait_recv()
            spread(partner, across, (on_out, on_in), at, start, size).start()

        def settle(at, start, size):
            spread(partner, partner, (near_out, near_in), at, start, size).wait()
            spread(across, me, (far_out, far_in), at, start, size).wait_send()
            spread(partner, diagonal, (on_out, on_in), at, start, size).wait()

        each(relay)
        each(settle)
    if summing:
        gift(0).wait_send()
        gift(1).wait_send()
        each(lambda at, start, size: crossing(at, start, size).wait_send())


def segment(number, middle, rows, vectors, outs, n_sums, product=None, sending=True,
            grouped=None):
    share, width = rows[0].shape
    flipped = None
    operands = []
    shapes = []
    scratch = []
    pieces = -(-share // STEP)
    places = lax.axis_size("tensor")
    flops = 0
    if product is not None:
        left, right, flipped = product
        operands += [left, right]
        flops = 2 * left.shape[0] * right.size
        scratch += [
            pltpu.VMEM((2, share, width), LOW),
            pltpu.VMEM((2, share, width), LOW),
            pltpu.VMEM((2, share, width), jnp.float32),
            pltpu.VMEM((share, width), LOW),
            pltpu.VMEM((share, width), LOW),
            pltpu.SemaphoreType.DMA((2,)),
            pltpu.SemaphoreType.DMA((2,)),
            pltpu.SemaphoreType.DMA((pieces,)),
            pltpu.SemaphoreType.DMA((pieces,)),
        ]
    operands += list(rows) + [vector.reshape(1, width) for vector in vectors]
    n_grouped = 0
    if grouped is not None:
        sources, small_shared, small_owned = grouped
        n_grouped = len(sources)
        n_shared = n_sums + small_shared.shape[0]
        operands += list(sources) + [small_shared, small_owned]
    if sending:
        shapes.append(jax.ShapeDtypeStruct((places * share, width), LOW))
        scratch += [pltpu.SemaphoreType.DMA((pieces,))] * 6
    shapes += [jax.ShapeDtypeStruct((share, width), dtype) for dtype in outs]
    if n_grouped:
        shapes += [jax.ShapeDtypeStruct(source.shape, LOW) for source in sources]
        shapes.append(jax.ShapeDtypeStruct((n_shared, width), jnp.float32))
        shapes.append(jax.ShapeDtypeStruct(small_owned.shape, jnp.float32))
        scratch += group_sum_scratch(sources) + small_sum_scratch(n_shared, small_owned)
    if n_sums:
        shapes.append(jax.ShapeDtypeStruct((n_sums, 8, width), jnp.float32))
    counts = (len(rows), len(vectors), len(outs), n_sums, n_grouped)
    in_vmem = pl.BlockSpec(memory_space=pltpu.VMEM)
    moved = sum(item.size * item.dtype.itemsize for item in operands + shapes)
    return pl.pallas_call(
        partial(segment_kernel, middle, counts, flipped, sending),
        out_shape=shapes,
        in_specs=[in_vmem] * len(operands),
        out_specs=[in_vmem] * len(shapes),
        scratch_shapes=scratch,
        compiler_params=pltpu.CompilerParams(
            collective_id=number, has_side_effects=True, vmem_limit_bytes=48 * 2**20
        ),
        cost_estimate=pl.CostEstimate(
            flops=flops + 25_000_000_000, bytes_accessed=moved, transcendentals=0
        ),
    )(*operands)


def gelu_back(inner_act, grad_act):
    _, pullback = jax.vjp(partial(jax.nn.gelu, approximate=True), inner_act)
    return pullback(grad_act)[0]


QUERIES = 256
FIRST = 128
PAIR = 2
SCALE = 1.0 / math.sqrt(HD)


def blocks_of(rows):
    return [(start, min(QUERIES, rows - start)) for start in range(0, rows, QUERIES)]


def key_pieces(start, size):
    if start == 0:
        return [(0, size, True, True)]
    pieces = [(0, FIRST, False, True)]
    if start > FIRST:
        pieces.append((FIRST, start, False, False))
    return pieces + [(start, start + size, True, False)]


def hide(values, key_axis, keys_from, queries_from, causal, first, length, hidden):
    if not (causal or first):
        return values
    keys = keys_from + lax.broadcasted_iota(jnp.int32, values.shape, key_axis)
    valid = None
    if causal:
        queries = queries_from + lax.broadcasted_iota(jnp.int32, values.shape, 1 - key_axis)
        valid = keys <= queries
    if first:
        real = (keys >= TEXT) | (keys < length)
        valid = real if valid is None else valid & real
    return jnp.where(valid, values, hidden)


def part_of(packed, head, part):
    start = (head * 3 + part) * HD
    return packed[:, start : start + HD]


def attend_kernel(lengths, packed_ref, context_ref, top_ref):
    length = lengths[pl.program_id(0)]
    packed = packed_ref[...]
    outs = []
    for head in range(PAIR):
        queries = part_of(packed, head, 0) * jnp.bfloat16(SCALE)
        keys, values = part_of(packed, head, 1), part_of(packed, head, 2)
        contexts = []
        for start, size in blocks_of(packed.shape[0]):
            mine = queries[start : start + size]
            pieces = key_pieces(start, size)
            scores = [
                hide(times_transposed(mine, keys[low:high]), 1, low, start, causal, first,
                     length, -1e30)
                for low, high, causal, first in pieces
            ]
            top = scores[0].max(axis=1, keepdims=True)
            for score in scores[1:]:
                top = jnp.maximum(top, score.max(axis=1, keepdims=True))
            raised = [jnp.exp(score - top) for score in scores]
            total = sum(part.sum(axis=1, keepdims=True) for part in raised)
            inverse = 1.0 / total
            context = sum(
                jnp.dot((part * inverse).astype(LOW), values[low:high],
                        preferred_element_type=jnp.float32)
                for part, (low, high, _, _) in zip(raised, pieces)
            )
            contexts.append(context)
            top_ref[0, 0, start : start + size, head : head + 1] = top + jnp.log(total)
        outs.append(jnp.concatenate(contexts, axis=0))
    context_ref[...] = jnp.concatenate(outs, axis=1).astype(LOW)


def attend_back_kernel(lengths, packed_ref, grad_ref, top_ref, out_ref, column_ref, *scratch):
    length = lengths[pl.program_id(0)]
    packed = packed_ref[...]
    grads = grad_ref[...]
    outs = []
    for head in range(PAIR):
        grad_keys, grad_values, grad_queries = scratch[3 * head : 3 * head + 3]
        queries = part_of(packed, head, 0) * jnp.bfloat16(SCALE)
        keys, values = part_of(packed, head, 1), part_of(packed, head, 2)
        grad = grads[:, head * HD : (head + 1) * HD]
        grad_keys[...] = jnp.zeros_like(grad_keys)
        grad_values[...] = jnp.zeros_like(grad_values)
        for start, size in blocks_of(packed.shape[0]):
            mine, grad_mine = queries[start : start + size], grad[start : start + size]
            top = top_ref[0, 0, head : head + 1, start : start + size]
            pieces = key_pieces(start, size)
            weights, products = [], []
            for low, high, causal, first in pieces:
                score = times_transposed(keys[low:high], mine)
                weight = jnp.exp(
                    hide(score, 0, low, start, causal, first, length, -1e30) - top
                )
                weights.append(weight)
                grad_values[low:high] += jnp.dot(
                    weight.astype(LOW), grad_mine, preferred_element_type=jnp.float32
                )
                products.append(times_transposed(values[low:high], grad_mine))
            mean = sum(
                (weight * product).sum(axis=0, keepdims=True)
                for weight, product in zip(weights, products)
            )
            turned = 0.0
            for (low, high, _, _), weight, product in zip(pieces, weights, products):
                grad_score = (weight * (product - mean)).astype(LOW)
                grad_keys[low:high] += jnp.dot(
                    grad_score, mine, preferred_element_type=jnp.float32
                )
                turned = turned + transposed_times(keys[low:high], grad_score)
            grad_queries[start : start + size] = turned.T * SCALE
        outs += [grad_queries[...], grad_keys[...], grad_values[...]]
    packed_grad = jnp.concatenate(outs, axis=1).astype(LOW)
    out_ref[...] = packed_grad
    column_ref[0, 0] = jnp.sum(packed_grad.astype(jnp.float32), axis=0, keepdims=True)


def attend(packed, lengths):
    sequences = lengths.shape[0]
    rows = packed.shape[0] // sequences
    pairs = packed.shape[1] // (3 * PAIR * HD)
    area = packed.shape[0] * rows * pairs * PAIR
    return pl.pallas_call(
        attend_kernel,
        grid=(sequences, pairs),
        in_specs=[
            pl.BlockSpec(memory_space=pltpu.SMEM),
            pl.BlockSpec((rows, 3 * PAIR * HD), lambda at, pair: (at, pair)),
        ],
        out_specs=[
            pl.BlockSpec((rows, PAIR * HD), lambda at, pair: (at, pair)),
            pl.BlockSpec((1, 1, rows, PAIR), lambda at, pair: (at, pair, 0, 0)),
        ],
        out_shape=[
            jax.ShapeDtypeStruct((packed.shape[0], pairs * PAIR * HD), LOW),
            jax.ShapeDtypeStruct((sequences, pairs, rows, PAIR), jnp.float32),
        ],
        cost_estimate=pl.CostEstimate(
            flops=8 * area * HD, bytes_accessed=3 * packed.size, transcendentals=area
        ),
        name="attend",
    )(lengths, packed)


def attend_back(packed, grad_context, tops, lengths):
    sequences = lengths.shape[0]
    rows = packed.shape[0] // sequences
    pairs = packed.shape[1] // (3 * PAIR * HD)
    area = packed.shape[0] * rows * pairs * PAIR
    return pl.pallas_call(
        attend_back_kernel,
        grid=(sequences, pairs),
        in_specs=[
            pl.BlockSpec(memory_space=pltpu.SMEM),
            pl.BlockSpec((rows, 3 * PAIR * HD), lambda at, pair: (at, pair)),
            pl.BlockSpec((rows, PAIR * HD), lambda at, pair: (at, pair)),
            pl.BlockSpec((1, 1, PAIR, rows), lambda at, pair: (at, pair, 0, 0)),
        ],
        out_specs=[
            pl.BlockSpec((rows, 3 * PAIR * HD), lambda at, pair: (at, pair)),
            pl.BlockSpec((1, 1, 1, 3 * PAIR * HD), lambda at, pair: (at, pair, 0, 0)),
        ],
        out_shape=[
            jax.ShapeDtypeStruct(packed.shape, LOW),
            jax.ShapeDtypeStruct((sequences, pairs, 1, 3 * PAIR * HD), jnp.float32),
        ],
        scratch_shapes=[pltpu.VMEM((rows, HD), jnp.float32)] * (3 * PAIR),
        cost_estimate=pl.CostEstimate(
            flops=20 * area * HD, bytes_accessed=5 * packed.size, transcendentals=area
        ),
        name="attend_back",
    )(lengths, packed, grad_context, tops)


def local(
    tokens,
    text_lengths,
    norm1_gain,
    norm1_shift,
    w_qkv,
    q_bias,
    v_bias,
    w_out,
    out_bias,
    norm2_gain,
    norm2_shift,
    norm3_gain,
    norm3_shift,
    w_fc1,
    fc1_bias,
    w_fc2,
    fc2_bias,
    norm4_gain,
    norm4_shift,
    cotangent,
):
    local_heads = q_bias.shape[0] // HD
    (gathered_first,) = segment(1, before_attention, [tokens], [norm1_gain, norm1_shift], [], 0)
    biases = jnp.stack(
        [q_bias.reshape(-1, HD), jnp.zeros((local_heads, HD)), v_bias.reshape(-1, HD)], axis=1
    ).reshape(1, -1)
    packed = (
        jnp.dot(gathered_first, w_qkv, preferred_element_type=jnp.float32) + biases
    ).astype(LOW)
    context_low, tops = attend(packed, text_lengths)
    gathered_third, branch, hidden = segment(
        2, after_attention, [tokens],
        [out_bias, norm2_gain, norm2_shift, norm3_gain, norm3_shift],
        [jnp.float32, jnp.float32], 0, (context_low, w_out, False),
    )
    inner_act = jnp.dot(gathered_third, w_fc1, preferred_element_type=jnp.float32) + fc1_bias
    activated = jax.nn.gelu(inner_act, approximate=True).astype(LOW)
    gathered_grad, layer_out, sums4 = segment(
        3, turn_round, [hidden, cotangent], [fc2_bias, norm4_gain, norm4_shift],
        [LOW], 3, (activated, w_fc2, False),
    )
    grad_activated = times_transposed(gathered_grad, w_fc2)
    ffn_fc2 = transposed_times(activated, gathered_grad)
    grad_inner = gelu_back(inner_act, grad_activated).astype(LOW)
    ffn_fc1_bias = jnp.sum(grad_inner, axis=0, dtype=jnp.float32)
    ffn_fc1 = transposed_times(gathered_third, grad_inner)
    grad_inner, ffn_fc1, ffn_fc2 = lax.optimization_barrier(
        (grad_inner, ffn_fc1.astype(LOW), ffn_fc2.astype(LOW))
    )
    ffn_fc1, ffn_fc2 = lax.psum((ffn_fc1, ffn_fc2), "dp")
    gathered_branch, grad_hidden, sums3 = segment(
        4, after_feed_forward, [branch, hidden, cotangent],
        [norm2_gain, norm3_gain], [jnp.float32], 5, (grad_inner, w_fc1, True),
    )
    grad_context = times_transposed(gathered_branch, w_out).astype(LOW)
    part_out = transposed_times(context_low, gathered_branch)
    grad_projected, columns = attend_back(
        packed, grad_context, tops.transpose(0, 1, 3, 2), text_lengths
    )
    columns = columns.sum(axis=0).reshape(local_heads, 3, HD)
    part_q_bias, part_v_bias = columns[:, 0].reshape(-1), columns[:, 2].reshape(-1)
    part_qkv = transposed_times(gathered_first, grad_projected)
    width = w_out.shape[1]
    depth = w_out.shape[0]
    folded_out = part_out.astype(LOW).reshape(depth, width // depth, depth)
    folded_out = folded_out.transpose(1, 0, 2).reshape(width, depth)
    owned = jnp.concatenate([part_q_bias, part_v_bias, ffn_fc1_bias])
    input_grad, part_qkv, folded_out, shared, owned, _ = segment(
        5, at_the_input, [tokens, grad_hidden], [norm1_gain], [jnp.float32], 2,
        (grad_projected, w_qkv, True), False,
        (
            [part_qkv.astype(LOW), folded_out],
            jnp.concatenate([sums3, sums4]),
            owned.reshape(-1, width // lax.axis_size("tensor")),
        ),
    )
    part_out = folded_out.reshape(width // depth, depth, depth).transpose(1, 0, 2)
    part_out = part_out.reshape(depth, width)
    (
        grad_gain1,
        grad_shift1,
        grad_gain3,
        grad_shift3,
        grad_gain2,
        grad_shift2,
        grad_out_bias,
        grad_gain4,
        grad_shift4,
        grad_fc2_bias,
    ) = shared
    owned = owned.reshape(-1)
    cuts = [part_q_bias.shape[0], part_q_bias.shape[0] + part_v_bias.shape[0]]
    part_q_bias, part_v_bias, ffn_fc1_bias = jnp.split(owned, cuts)
    part_qkv, part_out, ffn_fc1, ffn_fc2 = (
        total.astype(jnp.float32) for total in (part_qkv, part_out, ffn_fc1, ffn_fc2)
    )
    return (
        layer_out,
        input_grad,
        grad_gain1,
        grad_shift1,
        part_qkv,
        part_q_bias,
        part_v_bias,
        part_out,
        grad_out_bias,
        grad_gain2,
        grad_shift2,
        grad_gain3,
        grad_shift3,
        ffn_fc1,
        ffn_fc1_bias,
        ffn_fc2,
        grad_fc2_bias,
        grad_gain4,
        grad_shift4,
    )


def solution(mesh):
    in_specs = (
        P(("dp", "tensor"), None),
        P("dp"),
        P(),
        P(),
        P(None, "tensor"),
        P("tensor"),
        P("tensor"),
        P("tensor", None),
        P(),
        P(),
        P(),
        P(),
        P(),
        P(None, "tensor"),
        P("tensor"),
        P("tensor", None),
        P(),
        P(),
        P(),
        P(("dp", "tensor"), None),
    )
    out_specs = (
        P(("dp", "tensor"), None),
        P(("dp", "tensor"), None),
        P(),
        P(),
        P(None, "tensor"),
        P("tensor"),
        P("tensor"),
        P("tensor", None),
        P(),
        P(),
        P(),
        P(),
        P(),
        P(None, "tensor"),
        P("tensor"),
        P("tensor", None),
        P(),
        P(),
        P(),
    )
    return jax.shard_map(
        local, mesh=mesh, in_specs=in_specs, out_specs=out_specs, check_vma=False
    )
```

profile of v0, /device:TPU:0, one launch (start us, length us, event | category | flops | bytes accessed | tf_op | source)
XLA Modules:
  0.0 347.1 jit_solution(15118875210871819548)
XLA Ops:
  7.9 0.8 stack_reshape.6
  10.3 1.1 copy-done.6
  12.7 17.6 %shard_map.339 = bf16[1088,1024]{1,0:T(8,128)(2,1)S(1)} custom-call(bf16[272,1024]{1,0:T(8,128)(2,1)S(1)} %copy-done.6, f32[1,1024]{1,0:T(1,128)S(1)} %bitcast.69, f32[1,1024]{1,0:T(1,128)S(1)} %bitcast.58), custom_call_target="tpu_custom_call" | custom-call | flops 24999999488 | bytes 2793472 | tf_op jit(solution)/shard_map/pallas_call | solution.py:534
  30.4 1.4 copy-done.20
  31.7 3.1 fusion.7.packed_ref
  34.9 12.5 %attend.1 = (bf16[1088,256]{1,0:T(8,128)(2,1)}, f32[1,2,1088,2]{3,2,1,0:T(8,128)}) custom-call(s32[1]{0:T(128)S(6)} %copy.54.lengths, bf16[1088,768]{1,0:T(8,128)(2,1)} %fusion.7.packed_ref), custom_call_target="tpu_custom_call" | custom-call | flops 2424307712 | bytes 2506752 | tf_op jit(solution)/shard_map/attend/pallas_call | solution.py:675
  47.5 1.0 copy-done
  48.5 31.6 %shard_map.340 = (bf16[1088,1024]{1,0:T(8,128)(2,1)S(1)}, f32[272,1024]{1,0:T(8,128)S(1)}, f32[272,1024]{1,0:T(8,128)S(1)}) custom-call(bf16[1088,256]{1,0:T(8,128)(2,1)S(1)} %copy-done, bf16[256,1024]{1,0:T(8,128)(2,1)S(1)} %copy-done.8, bf16[272,1024]{1,0:T(8,128)(2,1)S(1)} %copy-done.7, f32[1,1024]{1,0:T(1,128)S(1)} %bitcast.59, f32[1,1024]{1,0:T(1,128)S(1)} %bitcast.65, ...), custom_call_target="tpu_custom_call" | custom-call | flops 25570424832 | bytes 6115328 | tf_op jit(solution)/shard_map/pallas_call | solution.py:534
  80.1 1.1 copy-done.23
  81.3 4.8 %multiply_convert_fusion = (bf16[1088,1024]{1,0:T(8,128)(2,1)}, f32[1088,1024]{1,0:T(8,128)S(1)}) fusion(f32[1024]{0:T(1024)S(1)} %convert_element_type.52, bf16[1088,1024]{1,0:T(8,128)(2,1)S(1)} %get-tuple-element.41, bf16[1024,1024]{1,0:T(8,128)(2,1)S(1)} %copy-done.3), kind=kOutput, calls=%fused_computation.11 | convolution fusion | flops 2292842496 | bytes 11014144 | tf_op jit(solution)/shard_map/dot_general | solution.py:763
  86.1 35.6 %shard_map.341 = (bf16[1088,1024]{1,0:T(8,128)(2,1)}, bf16[272,1024]{1,0:T(8,128)(2,1)S(1)}, f32[3,8,1024]{2,1,0:T(8,128)S(1)}) custom-call(bf16[1088,1024]{1,0:T(8,128)(2,1)} %get-tuple-element.79.refs_0_, bf16[1024,1024]{1,0:T(8,128)(2,1)S(1)} %copy-done.2, f32[272,1024]{1,0:T(8,128)S(1)} %get-tuple-element.42.refs_2_.refs_3_, ...), custom_call_target="tpu_custom_call" | custom-call | flops 27281700864 | bytes 8892416 | tf_op jit(solution)/shard_map/pallas_call | solution.py:534
  121.7 6.7 %convolution_convert_fusion.1 = bf16[1024,1024]{1,0:T(8,128)(2,1)} fusion(bf16[1088,1024]{1,0:T(8,128)(2,1)} %get-tuple-element.79.refs_0_, bf16[1088,1024]{1,0:T(8,128)(2,1)} %get-tuple-element.44), kind=kOutput, calls=%fused_computation.15 | convolution fusion | flops 2282749952 | bytes 6553600 | tf_op jit(solution)/shard_map/dot_general | solution.py:25
  128.5 5.4 %convert_reduce_fusion = (f32[1024]{0:T(1024)S(1)}, bf16[1088,1024]{1,0:T(8,128)(2,1)S(1)}) fusion(f32[1088,1024]{1,0:T(8,128)S(1)} %get-tuple-element.80, bf16[1088,1024]{1,0:T(8,128)(2,1)S(1)} %copy-done.31, bf16[1024,1024]{1,0:T(8,128)(2,1)S(1)} %copy-done.2), kind=kOutput, calls=%fused_computation.10 | convolution fusion | flops 2306210816 | bytes 11014144 | tf_op jit(solution)/shard_map/dot_general | solution.py:19
  133.8 1.4 copy-done.30
  135.2 4.1 %convolution_convert_fusion.2 = bf16[1024,1024]{1,0:T(8,128)(2,1)} fusion(bf16[1088,1024]{1,0:T(8,128)(2,1)S(1)} %get-tuple-element.41, bf16[1088,1024]{1,0:T(8,128)(2,1)S(1)} %get-tuple-element.45.refs_0_), kind=kOutput, calls=%fused_computation.16 | convolution fusion | flops 2282749952 | bytes 6553600 | tf_op jit(solution)/shard_map/dot_general | solution.py:25
  139.3 1.6 copy-done.4
  140.9 1.2 copy-done.24
  142.2 1.2 copy-done.26
  143.4 35.8 %shard_map.342 = (bf16[1088,1024]{1,0:T(8,128)(2,1)}, f32[272,1024]{1,0:T(8,128)S(1)}, f32[5,8,1024]{2,1,0:T(8,128)S(1)}) custom-call(bf16[1088,1024]{1,0:T(8,128)(2,1)} %copy-done.30, bf16[1024,1024]{1,0:T(8,128)(2,1)S(1)} %copy-done.4, f32[272,1024]{1,0:T(8,128)S(1)} %copy-done.24, f32[272,1024]{1,0:T(8,128)S(1)} %copy-done.26, ...), custom_call_target="tpu_custom_call" | custom-call | flops 27281700864 | bytes 10625024 | tf_op jit(solution)/shard_map/pallas_call | solution.py:534
  179.3 3.0 convolution_convert_fusion.4
  182.3 1.6 convolution_convert_fusion.grad_ref
  183.8 2.2 copy.42
  186.1 19.2 %attend_back.1 = (bf16[1088,768]{1,0:T(8,128)(2,1)}, f32[1,2,1,384]{3,2,1,0:T(1,128)}) custom-call(s32[1]{0:T(128)S(6)} %copy.54.lengths, bf16[1088,768]{1,0:T(8,128)(2,1)} %fusion.7.packed_ref, bf16[1088,256]{1,0:T(8,128)(2,1)} %convolution_convert_fusion.grad_ref, f32[1,2,2,1088]{3,2,1,0:T(2,128)} %bitcast.73), custom_call_target="tpu_custom_call" | custom-call | flops 6060769280 | bytes 4177920 | tf_op jit(solution)/shard_map/attend_back/pallas_call | solution.py:702
  206.4 5.6 %convolution_convert_fusion.3.refs_5_ = bf16[1024,768]{1,0:T(8,128)(2,1)} fusion(bf16[1088,1024]{1,0:T(8,128)(2,1)} %copy-done.20, bf16[1088,768]{1,0:T(8,128)(2,1)} %get-tuple-element.49.refs_0_), kind=kOutput, calls=%fused_computation.17 | convolution fusion | flops 1712062464 | bytes 5472256 | tf_op jit(solution)/shard_map/dot_general | solution.py:25
  212.1 113.9 %shard_map.343 = (f32[272,1024]{1,0:T(8,128)S(1)}, bf16[1024,768]{1,0:T(8,128)(2,1)S(1)}, bf16[1024,256]{1,0:T(8,128)(2,1)S(1)}, f32[10,1024]{1,0:T(8,128)S(1)},...) custom-call(bf16[1088,768]{1,0:T(8,128)(2,1)} %get-tuple-element.49.refs_0_, bf16[1024,768]{1,0:T(8,128)(2,1)} %refs_1_.7, ...), custom_call_target="tpu_custom_call" | custom-call | flops 26711275520 | bytes 10608640 | tf_op jit(solution)/shard_map/pallas_call | solution.py:534
  326.7 1.1 copy.46
  327.8 1.9 convert_element_type.61
  330.9 0.8 all-reduce.3.cloned.1.call-done
  331.7 4.2 %convert_element_type.66 = f32[1024,1024]{1,0:T(8,128)} convert(bf16[1024,1024]{1,0:T(8,128)(2,1)} %get-tuple-element.63) | non-fusion elementwise | flops 1048576 | bytes 6291456 | tf_op jit(solution)/shard_map/convert_element_type | solution.py:822
  336.0 2.5 convert_element_type.67
  338.4 0.8 copy.55
  339.2 1.0 copy.56
  (77 shorter events, 6.2 us)
Async XLA Ops:
  7.2 324.5 %all-reduce.3.cloned.1.call-start = ((), (), s32[]{:S(2)}) async-start(), calls=%async_computation | async-start | bytes 8388608 | tf_op jit(solution)/shard_map/psum | solution.py:777
  10.3 1.1 copy-start.6
  11.4 0.7 copy-start.9
  12.7 19.0 %copy-start.29 = (bf16[1024,768]{1,0:T(8,128)(2,1)S(1)}, bf16[1024,768]{1,0:T(8,128)(2,1)}, u32[]{:S(2)}) copy-start(bf16[1024,768]{1,0:T(8,128)(2,1)} %refs_1_.7) | copy-start | bytes 4718596
  30.4 1.4 copy-start.20
  34.8 12.6 %copy-start.7 = (bf16[272,1024]{1,0:T(8,128)(2,1)S(1)}, bf16[272,1024]{1,0:T(8,128)(2,1)}, u32[]{:S(2)}) copy-start(bf16[272,1024]{1,0:T(8,128)(2,1)} %refs_2_.3) | copy-start | bytes 1671172
  34.8 12.6 %copy-start.8 = (bf16[256,1024]{1,0:T(8,128)(2,1)S(1)}, bf16[256,1024]{1,0:T(8,128)(2,1)}, u32[]{:S(2)}) copy-start(bf16[256,1024]{1,0:T(8,128)(2,1)} %refs_1_.4) | copy-start | bytes 1572868
  34.8 12.6 %copy-start.10 = (f32[1024]{0:T(1024)S(1)}, f32[1024]{0:T(1024)}, u32[]{:S(2)}) copy-start(f32[1024]{0:T(1024)} %param.28) | copy-start | bytes 12292
  34.8 12.6 %copy-start.11 = (f32[1024]{0:T(1024)S(1)}, f32[1024]{0:T(1024)}, u32[]{:S(2)}) copy-start(f32[1024]{0:T(1024)} %param.30) | copy-start | bytes 12292
  34.8 12.6 %copy-start.12 = (f32[1024]{0:T(1024)S(1)}, f32[1024]{0:T(1024)}, u32[]{:S(2)}) copy-start(f32[1024]{0:T(1024)} %param.32) | copy-start | bytes 12292
  34.9 12.6 %copy-start.16 = (f32[1024]{0:T(1024)S(1)}, f32[1024]{0:T(1024)}, u32[]{:S(2)}) copy-start(f32[1024]{0:T(1024)} %param.29) | copy-start | bytes 12292
  34.9 12.6 %copy-start.17 = (f32[1024]{0:T(1024)S(1)}, f32[1024]{0:T(1024)}, u32[]{:S(2)}) copy-start(f32[1024]{0:T(1024)} %param.31) | copy-start | bytes 12292
  47.5 1.1 copy-start
  48.5 32.7 %copy-start.3 = (bf16[1024,1024]{1,0:T(8,128)(2,1)S(1)}, bf16[1024,1024]{1,0:T(8,128)(2,1)}, u32[]{:S(2)}) copy-start(bf16[1024,1024]{1,0:T(8,128)(2,1)} %refs_1_.6) | copy-start | bytes 6291460
  80.1 1.1 copy-start.23
  81.2 4.9 %copy-start.25 = (f32[272,1024]{1,0:T(8,128)}, f32[272,1024]{1,0:T(8,128)S(1)}, u32[]{:S(2)}) copy-start(f32[272,1024]{1,0:T(8,128)S(1)} %get-tuple-element.42.refs_2_.refs_3_) | copy-start | bytes 3342340
  81.2 4.8 %copy-start.2 = (bf16[1024,1024]{1,0:T(8,128)(2,1)S(1)}, bf16[1024,1024]{1,0:T(8,128)(2,1)}, u32[]{:S(2)}) copy-start(bf16[1024,1024]{1,0:T(8,128)(2,1)} %refs_1_.5) | copy-start | bytes 6291460
  81.2 4.8 %copy-start.5 = (bf16[272,1024]{1,0:T(8,128)(2,1)S(1)}, bf16[272,1024]{1,0:T(8,128)(2,1)}, u32[]{:S(2)}) copy-start(bf16[272,1024]{1,0:T(8,128)(2,1)} %refs_4_.1) | copy-start | bytes 1671172
  81.2 4.8 %copy-start.13 = (f32[1024]{0:T(1024)S(1)}, f32[1024]{0:T(1024)}, u32[]{:S(2)}) copy-start(f32[1024]{0:T(1024)} %param.36) | copy-start | bytes 12292
  81.2 4.8 %copy-start.14 = (f32[1024]{0:T(1024)S(1)}, f32[1024]{0:T(1024)}, u32[]{:S(2)}) copy-start(f32[1024]{0:T(1024)} %param.37) | copy-start | bytes 12292
  81.3 4.8 %copy-start.15 = (f32[1024]{0:T(1024)S(1)}, f32[1024]{0:T(1024)}, u32[]{:S(2)}) copy-start(f32[1024]{0:T(1024)} %param.38) | copy-start | bytes 12292
  121.7 6.8 %copy-start.31 = (bf16[1088,1024]{1,0:T(8,128)(2,1)S(1)}, bf16[1088,1024]{1,0:T(8,128)(2,1)}, u32[]{:S(2)}) copy-start(bf16[1088,1024]{1,0:T(8,128)(2,1)} %get-tuple-element.44) | copy-start | bytes 6684676
  133.8 1.4 copy-start.30
  139.3 1.6 copy-start.4
  140.9 1.2 copy-start.24
  142.2 1.2 copy-start.26
  143.4 35.8 %copy-start.1 = (bf16[1088,256]{1,0:T(8,128)(2,1)S(1)}, bf16[1088,256]{1,0:T(8,128)(2,1)}, u32[]{:S(2)}) copy-start(bf16[1088,256]{1,0:T(8,128)(2,1)} %get-tuple-element.40.refs_0_) | copy-start | bytes 1671172
  179.2 4.6 %copy-start.21 = (f32[272,1024]{1,0:T(8,128)}, f32[272,1024]{1,0:T(8,128)S(1)}, u32[]{:S(2)}) copy-start(f32[272,1024]{1,0:T(8,128)S(1)} %get-tuple-element.50.refs_3_) | copy-start | bytes 3342340
  179.2 3.0 copy-start.27
  206.4 5.7 %copy-start.19 = (f32[1024]{0:T(1024)S(1)}, f32[1024]{0:T(1024)}, u32[]{:S(2)}) copy-start(f32[1024]{0:T(1024)} %param.22) | copy-start | bytes 12292
  206.4 5.7 %copy-start.22 = (f32[272,1024]{1,0:T(8,128)S(1)}, f32[272,1024]{1,0:T(8,128)}, u32[]{:S(2)}) copy-start(f32[272,1024]{1,0:T(8,128)} %copy-done.21) | copy-start | bytes 3342340
  331.7 4.2 %copy-start.28 = (bf16[1024,1024]{1,0:T(8,128)(2,1)S(1)}, bf16[1024,1024]{1,0:T(8,128)(2,1)}, u32[]{:S(2)}) copy-start(bf16[1024,1024]{1,0:T(8,128)(2,1)} %get-tuple-element.64) | copy-start | bytes 6291460
  (1 other events, 0.7 us)
Sparse Core Ops, SparseCore 0:
  139.4 192.2 all-reduce.2
where the time goes:
time: 349 us; the launch traced here: 347 us
  Pallas kernels  266 us (76%)
  matrix products  34.3 us (10%)
  local copies, waits for them, and re-layouts  20.4 us (6%)
  between operations  15 us (4%)
  other arithmetic  10.2 us (3%)
    pallas_call x5, Pallas kernels, segment(): pl.pallas_call(partial(segment_kernel, middle, counts, flipped, sending),...  235 us
    dot_general x4, matrix products, transposed_times(): lax.dot_general(left, right, (((0,), (0,)), ((), ())), preferred_element_...  19.5 us
    pallas_call x1, Pallas kernels, attend_back(): pl.pallas_call(attend_back_kernel, grid=(sequences, pairs), in_specs=[pl....  19.2 us
    unnamed x68, local copies, waits for them, and re-layouts  13.8 us
    pallas_call x1, Pallas kernels, attend(): pl.pallas_call(attend_kernel, grid=(sequences, pairs), in_specs=[pl.Block...  12.5 us
    convert_element_type x3, other arithmetic, local(): total.astype(jnp.float32)  8.59 us
  transfers between devices with their start and end apart: 1, of which 1 were waited for; matrix products, arithmetic and copies ran while one was open for 5% of the time, Pallas kernels for 49%

commit v1 on v0

--- a/solution.py
+++ b/solution.py
@@ -29,6 +29,7 @@
 
 STEP = 64
 TILE = 256
+FINISH_AT = 14.0
 MESH = pl.DeviceIdType.MESH
 LOW = jnp.bfloat16
 
@@ -87,42 +88,39 @@
 
 
 class GroupSum:
-    def __init__(self, sources, results, scratch):
-        self.kept, self.near, self.far = scratch[:3]
-        self.sems = scratch[3:]
+    def __init__(self, sources, results, scratch, scatter=True, gather=True):
+        self.scatter, self.gather = scatter, gather
+        scratch = list(scratch)
+        if scatter:
+            self.kept, self.fresh, self.half_out, self.half_in = scratch[:4]
+            scratch = scratch[4:]
+        if gather:
+            self.join_out, self.join_in = scratch
         self.sources, self.results = sources, results
+        groups = lax.axis_size("dp")
+        self.stages = groups.bit_length() - 1
+        self.depth = sources[0].shape[0] if scatter else results[0].shape[0]
         self.pieces = [
             (at, column)
             for at, source in enumerate(sources)
             for column in range(0, source.shape[1], TILE)
         ]
-        self.half = sources[0].shape[0] // 2
-        self.peers = lax.axis_size("dp") // 2
-        self.part = self.half // self.peers
-        group = lax.axis_index("dp")
-        self.side = lax.rem(group, 2)
-        self.place = lax.div(group, 2)
-        self.partner = group + 1 - 2 * self.side
-
-    def others(self):
-        for hop in range(1, self.peers):
-            yield (
-                hop - 1,
-                lax.rem(self.place + hop, self.peers),
-                lax.rem(self.place + self.peers - hop, self.peers),
-            )
-
-    def device(self, place):
-        return place * 2 + self.side
-
-    def targets(self):
-        return [self.partner] + [self.device(ahead) for _, ahead, _ in self.others()]
-
-    def send(self, source, target, outgoing, incoming, device):
-        return pltpu.make_async_remote_copy(
-            source, target, outgoing, incoming,
-            device_id={"dp": device}, device_id_type=MESH,
-        )
+        self.group = lax.axis_index("dp")
+        self.routes = [self.route() for _ in range(len(self.pieces))]
+
+    def partner(self, bit):
+        side = lax.rem(lax.div(self.group, 2**bit), 2)
+        return side, self.group + (1 - 2 * side) * 2**bit
+
+    def route(self):
+        bits = list(range(self.stages))
+        start, size, route = 0, self.depth, []
+        for bit in bits:
+            side, partner = self.partner(bit)
+            size //= 2
+            route.append((partner, start + side * size, start + (1 - side) * size, size))
+            start = start + side * size
+        return route
 
     def rows(self, start, size):
         return pl.ds(pl.multiple_of(start, 16), size)
@@ -131,83 +129,96 @@
         at, column = self.pieces[piece]
         return self.sources[at], self.results[at], pl.ds(column, TILE), pl.ds(piece * TILE, TILE)
 
-    def halving(self, piece):
+    def halving(self, piece, stage):
         source, _, cut, held = self.cuts(piece)
-        return self.send(
-            source.at[self.rows((1 - self.side) * self.half, self.half), cut],
-            self.near.at[:, held], self.sems[0].at[piece], self.sems[1].at[piece], self.partner,
+        partner, _, given, size = self.routes[piece][stage]
+        given = self.rows(given, size)
+        return pltpu.make_async_remote_copy(
+            self.kept.at[given, held] if stage else source.at[given, cut],
+            self.fresh.at[pl.ds(self.depth - 2 * size, size), held],
+            self.half_out.at[stage, piece], self.half_in.at[stage, piece],
+            device_id={"dp": partner}, device_id_type=MESH,
         )
 
-    def parting(self, piece, slot, ahead):
-        held = pl.ds(piece * TILE, TILE)
-        return self.send(
-            self.kept.at[self.rows(ahead * self.part, self.part), held], self.far.at[slot, :, held],
-            self.sems[2].at[slot, piece], self.sems[3].at[slot, piece], self.device(ahead),
-        )
-
-    def joining(self, piece, slot, owner, ahead):
-        _, result, cut, _ = self.cuts(piece)
-        region = result.at[self.rows(self.side * self.half + owner * self.part, self.part), cut]
-        return self.send(
-            region, region, self.sems[4].at[slot, piece], self.sems[5].at[slot, piece],
-            self.device(ahead),
-        )
-
-    def doubling(self, piece, side):
-        _, result, cut, _ = self.cuts(piece)
-        region = result.at[self.rows(side * self.half, self.half), cut]
-        return self.send(
-            region, region, self.sems[6].at[piece], self.sems[7].at[piece], self.partner
+    def joining(self, piece, stage, arriving=False):
+        source, result, cut, _ = self.cuts(piece)
+        partner, kept, given, size = self.routes[piece][stage]
+        region = result.at[self.rows(given if arriving else kept, size), cut]
+        first = stage == self.stages - 1 and not self.scatter
+        return pltpu.make_async_remote_copy(
+            source.at[:, cut] if first else region, region,
+            self.join_out.at[stage, piece], self.join_in.at[stage, piece],
+            device_id={"dp": partner}, device_id_type=MESH,
         )
 
     def start(self):
         for piece in range(len(self.pieces)):
-            self.halving(piece).start()
-
-    def after_halving(self, piece):
-        source, _, cut, held = self.cuts(piece)
-        self.halving(piece).wait_recv()
-        mine = source[self.rows(self.side * self.half, self.half), cut].astype(jnp.float32)
-        self.kept[:, held] = (mine + self.near[:, held].astype(jnp.float32)).astype(LOW)
-        for slot, ahead, _ in self.others():
-            self.parting(piece, slot, ahead).start()
-
-    def after_parting(self, piece):
-        _, result, cut, held = self.cuts(piece)
-        total = self.kept[self.rows(self.place * self.part, self.part), held].astype(jnp.float32)
-        for slot, ahead, _ in self.others():
-            self.parting(piece, slot, ahead).wait_recv()
-            total = total + self.far[slot, :, held].astype(jnp.float32)
-        own = self.rows(self.side * self.half + self.place * self.part, self.part)
-        result[own, cut] = total.astype(LOW)
-        for slot, ahead, _ in self.others():
-            self.joining(piece, slot, self.place, ahead).start()
-
-    def after_joining(self, piece):
-        for slot, ahead, behind in self.others():
-            self.joining(piece, slot, behind, ahead).wait_recv()
-        self.doubling(piece, self.side).start()
-
-    def settle(self, piece):
-        self.doubling(piece, 1 - self.side).wait_recv()
-        self.doubling(piece, self.side).wait_send()
-        self.halving(piece).wait_send()
-        for slot, ahead, _ in self.others():
-            self.parting(piece, slot, ahead).wait_send()
-            self.joining(piece, slot, self.place, ahead).wait_send()
-
-
-def group_sum_scratch(sources):
+            self.halving(piece, 0).start()
+
+    def start_joining(self):
+        for piece in range(len(self.pieces)):
+            self.joining(piece, self.stages - 1).start()
+        for piece in range(len(self.pieces)):
+            source, result, cut, _ = self.cuts(piece)
+            _, kept, _, size = self.routes[piece][-1]
+            result[self.rows(kept, size), cut] = source[:, cut]
+
+    def after_halving(self, piece, stage):
+        source, result, cut, held = self.cuts(piece)
+        _, kept, _, size = self.routes[piece][stage]
+        own = self.rows(kept, size)
+        self.halving(piece, stage).wait_recv()
+        mine = self.kept[own, held] if stage else source[own, cut]
+        arrived = self.fresh[pl.ds(self.depth - 2 * size, size), held]
+        total = (mine.astype(jnp.float32) + arrived.astype(jnp.float32)).astype(LOW)
+        if stage + 1 < self.stages:
+            self.kept[own, held] = total
+            self.halving(piece, stage + 1).start()
+        elif self.gather:
+            result[own, cut] = total
+            self.joining(piece, stage).start()
+        else:
+            result[:, cut] = total
+
+    def after_joining(self, piece, stage):
+        self.joining(piece, stage, True).wait_recv()
+        if stage:
+            self.joining(piece, stage - 1).start()
+
+    def settle(self):
+        for piece in range(len(self.pieces)):
+            for stage in range(self.stages):
+                if self.scatter:
+                    self.halving(piece, stage).wait_send()
+                if self.gather:
+                    self.joining(piece, stage).wait_send()
+
+    def scatter_steps(self, pace, hop, begin=0.0):
+        for piece in range(len(self.pieces)):
+            for stage in range(self.stages):
+                when = begin + pace * (piece + 1) + hop * stage
+                yield when, partial(self.after_halving, piece, stage)
+
+    def gather_steps(self, pace, hop, begin=0.0):
+        for piece in range(len(self.pieces)):
+            for stage in range(self.stages):
+                late = 0.0 if stage else 1000.0
+                when = begin + late + pace * (piece + 1) + hop * (self.stages - 1 - stage)
+                yield when, partial(self.after_joining, piece, stage)
+
+
+def in_turn(steps):
+    for _, step in sorted(steps, key=lambda item: item[0]):
+        step()
+
+
+def group_sum_scratch(sources, scatter=True, gather=True):
     pieces = sum(source.shape[1] for source in sources) // TILE
-    half = sources[0].shape[0] // 2
-    peers = lax.axis_size("dp") // 2
+    depth = sources[0].shape[0]
     width = pieces * TILE
-    pair, fan = pltpu.SemaphoreType.DMA((pieces,)), pltpu.SemaphoreType.DMA((peers - 1, pieces))
-    return [
-        pltpu.VMEM((half, width), LOW),
-        pltpu.VMEM((half, width), LOW),
-        pltpu.VMEM((peers - 1, half // peers, width), LOW),
-    ] + [pair, pair, fan, fan, fan, fan, pair, pair]
+    sems = pltpu.SemaphoreType.DMA((lax.axis_size("dp").bit_length() - 1, pieces))
+    held = [pltpu.VMEM((depth, width), LOW), pltpu.VMEM((depth, width), LOW), sems, sems]
+    return (held if scatter else []) + ([sems, sems] if gather else [])
 
 
 class SmallSum:
@@ -303,7 +314,7 @@
 
 
 def segment_kernel(middle, counts, flipped, sending, *refs):
-    n_rows, n_vectors, n_outs, n_sums, n_grouped = counts
+    n_rows, n_vectors, n_outs, n_sums, n_grouped, n_parted, n_joined = counts
     refs = list(refs)
 
     def take(count):
@@ -318,19 +329,28 @@
     if n_grouped:
         group_sources = take(n_grouped)
         small_in = take(2)
+        joined_sources = take(n_joined)
+    if n_parted:
+        group_sources = take(n_parted)
     gathered = take(1)[0] if sending else None
     out_refs = take(n_outs)
     if n_grouped:
         group_results = take(n_grouped)
         small_out = take(2)
+        joined_results = take(n_joined)
+    if n_parted:
+        group_results = take(n_parted)
     sums = take(1)[0] if n_sums else None
     if summing:
         give, got, keep, onward, came, give_sem, got_sem, out_sem, in_sem = take(9)
     if sending:
         near_out, near_in, far_out, far_in, on_out, on_in = take(6)
     if n_grouped:
-        grouped = GroupSum(group_sources, group_results, take(11))
+        grouped = GroupSum(group_sources, group_results, take(6))
         small = SmallSum(*small_in, sums, *small_out, *take(12))
+        joined = GroupSum(joined_sources, joined_results, take(2), False, True)
+    if n_parted:
+        grouped = GroupSum(group_sources, group_results, take(4), True, False)
 
     me = lax.axis_index("tensor")
     partner = me + 1 - 2 * lax.rem(me, 2)
@@ -359,6 +379,13 @@
         for other in small.others:
             pl.semaphore_signal(barrier, inc=1, device_id={"dp": other}, device_id_type=MESH)
         pl.semaphore_wait(barrier, 3 + len(small.others))
+        grouped.start()
+        joined.start_joining()
+    elif n_parted:
+        for bit in range(grouped.stages):
+            _, other = grouped.partner(bit)
+            pl.semaphore_signal(barrier, inc=1, device_id={"dp": other}, device_id_type=MESH)
+        pl.semaphore_wait(barrier, 2 + grouped.stages)
         grouped.start()
     else:
         pl.semaphore_wait(barrier, 2)
@@ -441,30 +468,24 @@
             spread(across, me, (far_out, far_in), at, start, size).start()
             spread(partner, me, (near_out, near_in), at, start, size).start()
 
+    steps = [(FINISH_AT, partial(each, finish))]
     if n_grouped:
-        pieces = len(grouped.pieces)
-        early = pieces // 2
-        for piece in range(early):
-            grouped.after_halving(piece)
-        each(finish)
-        small.first_send()
-        for piece in range(early, pieces):
-            grouped.after_halving(piece)
-            grouped.after_parting(piece - early)
-        small.first_wait()
-        small.second_send()
-        for piece in range(pieces - early, pieces):
-            grouped.after_joining(piece - (pieces - early))
-            grouped.after_parting(piece)
-        small.second_wait()
-        small.third_send()
-        for piece in range(early, pieces):
-            grouped.after_joining(piece)
-        small.third_wait()
-        for piece in range(pieces):
-            grouped.settle(piece)
-    else:
-        each(finish)
+        steps += list(grouped.scatter_steps(6.0, 12.0))
+        steps += list(grouped.gather_steps(6.0, 6.0, 36.0))
+        steps += list(joined.gather_steps(4.0, 4.0))
+        steps += [
+            (FINISH_AT + 0.5, small.first_send),
+            (FINISH_AT + 8, small.first_wait),
+            (FINISH_AT + 8, small.second_send),
+            (FINISH_AT + 30, small.second_wait),
+            (FINISH_AT + 30, small.third_send),
+            (1000.0, small.third_wait),
+            (2000.0, grouped.settle),
+            (2000.0, joined.settle),
+        ]
+    elif n_parted:
+        steps += list(grouped.scatter_steps(6.0, 5.0))
+        steps.append((2000.0, grouped.settle))
 
     if sending:
 
@@ -477,8 +498,8 @@
             spread(across, me, (far_out, far_in), at, start, size).wait_send()
             spread(partner, diagonal, (on_out, on_in), at, start, size).wait()
 
-        each(relay)
-        each(settle)
+        steps += [(FINISH_AT + 14, partial(each, relay)), (1500.0, partial(each, settle))]
+    in_turn(steps)
     if summing:
         gift(0).wait_send()
         gift(1).wait_send()
@@ -486,7 +507,7 @@
 
 
 def segment(number, middle, rows, vectors, outs, n_sums, product=None, sending=True,
-            grouped=None):
+            grouped=None, parted=()):
     share, width = rows[0].shape
     flipped = None
     operands = []
@@ -511,12 +532,15 @@
             pltpu.SemaphoreType.DMA((pieces,)),
         ]
     operands += list(rows) + [vector.reshape(1, width) for vector in vectors]
-    n_grouped = 0
+    n_grouped = n_joined = 0
     if grouped is not None:
-        sources, small_shared, small_owned = grouped
+        sources, small_shared, small_owned, joined = grouped
+        n_joined = len(joined)
         n_grouped = len(sources)
         n_shared = n_sums + small_shared.shape[0]
-        operands += list(sources) + [small_shared, small_owned]
+        operands += list(sources) + [small_shared, small_owned] + list(joined)
+    n_parted = len(parted)
+    operands += list(parted)
     if sending:
         shapes.append(jax.ShapeDtypeStruct((places * share, width), LOW))
         scratch += [pltpu.SemaphoreType.DMA((pieces,))] * 6
@@ -525,10 +549,21 @@
         shapes += [jax.ShapeDtypeStruct(source.shape, LOW) for source in sources]
         shapes.append(jax.ShapeDtypeStruct((n_shared, width), jnp.float32))
         shapes.append(jax.ShapeDtypeStruct(small_owned.shape, jnp.float32))
+        groups = lax.axis_size("dp")
+        shapes += [
+            jax.ShapeDtypeStruct((item.shape[0] * groups, item.shape[1]), LOW) for item in joined
+        ]
         scratch += group_sum_scratch(sources) + small_sum_scratch(n_shared, small_owned)
+        scratch += group_sum_scratch(joined, False, True)
+    if n_parted:
+        groups = lax.axis_size("dp")
+        shapes += [
+            jax.ShapeDtypeStruct((item.shape[0] // groups, item.shape[1]), LOW) for item in parted
+        ]
+        scratch += group_sum_scratch(parted, True, False)
     if n_sums:
         shapes.append(jax.ShapeDtypeStruct((n_sums, 8, width), jnp.float32))
-    counts = (len(rows), len(vectors), len(outs), n_sums, n_grouped)
+    counts = (len(rows), len(vectors), len(outs), n_sums, n_grouped, n_parted, n_joined)
     in_vmem = pl.BlockSpec(memory_space=pltpu.VMEM)
     moved = sum(item.size * item.dtype.itemsize for item in operands + shapes)
     return pl.pallas_call(
@@ -766,18 +801,17 @@
         3, turn_round, [hidden, cotangent], [fc2_bias, norm4_gain, norm4_shift],
         [LOW], 3, (activated, w_fc2, False),
     )
+    ffn_fc2 = transposed_times(activated, gathered_grad).astype(LOW)
+    gathered_grad, ffn_fc2 = lax.optimization_barrier((gathered_grad, ffn_fc2))
+    ffn_fc2 = lax.psum(ffn_fc2, "dp")
     grad_activated = times_transposed(gathered_grad, w_fc2)
-    ffn_fc2 = transposed_times(activated, gathered_grad)
     grad_inner = gelu_back(inner_act, grad_activated).astype(LOW)
     ffn_fc1_bias = jnp.sum(grad_inner, axis=0, dtype=jnp.float32)
-    ffn_fc1 = transposed_times(gathered_third, grad_inner)
-    grad_inner, ffn_fc1, ffn_fc2 = lax.optimization_barrier(
-        (grad_inner, ffn_fc1.astype(LOW), ffn_fc2.astype(LOW))
-    )
-    ffn_fc1, ffn_fc2 = lax.psum((ffn_fc1, ffn_fc2), "dp")
-    gathered_branch, grad_hidden, sums3 = segment(
+    ffn_fc1 = transposed_times(gathered_third, grad_inner).astype(LOW)
+    gathered_branch, grad_hidden, ffn_fc1, sums3 = segment(
         4, after_feed_forward, [branch, hidden, cotangent],
-        [norm2_gain, norm3_gain], [jnp.float32], 5, (grad_inner, w_fc1, True),
+        [norm2_gain, norm3_gain], [jnp.float32], 5, (grad_inner, w_fc1, True), True, None,
+        [ffn_fc1],
     )
     grad_context = times_transposed(gathered_branch, w_out).astype(LOW)
     part_out = transposed_times(context_low, gathered_branch)
@@ -792,13 +826,14 @@
     folded_out = part_out.astype(LOW).reshape(depth, width // depth, depth)
     folded_out = folded_out.transpose(1, 0, 2).reshape(width, depth)
     owned = jnp.concatenate([part_q_bias, part_v_bias, ffn_fc1_bias])
-    input_grad, part_qkv, folded_out, shared, owned, _ = segment(
+    input_grad, part_qkv, folded_out, shared, owned, ffn_fc1, _ = segment(
         5, at_the_input, [tokens, grad_hidden], [norm1_gain], [jnp.float32], 2,
         (grad_projected, w_qkv, True), False,
         (
             [part_qkv.astype(LOW), folded_out],
             jnp.concatenate([sums3, sums4]),
             owned.reshape(-1, width // lax.axis_size("tensor")),
+            [ffn_fc1],
         ),
     )
     part_out = folded_out.reshape(width // depth, depth, depth).transpose(1, 0, 2)

time: 349 us -> 331 us (0.948)
  Pallas kernels: 266 us -> 254 us
  local copies, waits for them, and re-layouts: 20.4 us -> 14.5 us
    pallas_call x5, Pallas kernels: 235 us -> 222 us  [segment(): pl.pallas_call(partial(segment_kernel, middle, counts, flipped, sending),...]
    unnamed x68 -> x76, local copies, waits for them, and re-layouts: 13.8 us -> 9.26 us
  transfers between devices with their start and end apart: 1 -> 1, of which waited for: 1 -> 0; matrix products, arithmetic and copies ran while one was open for 5% -> 9% of each run, Pallas kernels for 49% -> 47%
where the time goes in v1:
time: 331 us
  Pallas kernels  254 us (77%)
  matrix products  37.4 us (11%)
  between operations  15.2 us (5%)
  local copies, waits for them, and re-layouts  14.5 us (4%)
  other arithmetic  9.33 us (3%)
    pallas_call x5, Pallas kernels, segment(): pl.pallas_call(partial(segment_kernel, middle, counts, flipped, sending),...  222 us
    pallas_call x1, Pallas kernels, attend_back(): pl.pallas_call(attend_back_kernel, grid=(sequences, pairs), in_specs=[pl....  19.5 us
    dot_general x4, matrix products, transposed_times(): lax.dot_general(left, right, (((0,), (0,)), ((), ())), preferred_element_...  18.7 us
    pallas_call x1, Pallas kernels, attend(): pl.pallas_call(attend_kernel, grid=(sequences, pairs), in_specs=[pl.Block...  12.5 us
    dot_general x2, matrix products, times_transposed(): lax.dot_general(left, right, (((1,), (1,)), ((), ())), preferred_element_...  9.35 us
    unnamed x76, local copies, waits for them, and re-layouts  9.26 us
    convert_element_type x3, other arithmetic, local(): total.astype(jnp.float32)  8.44 us
  transfers between devices with their start and end apart: 1, of which 0 were waited for; matrix products, arithmetic and copies ran while one was open for 9% of the time, Pallas kernels for 47%

profile of v1, /device:TPU:0, one launch (start us, length us, event | category | flops | bytes accessed | tf_op | source)
XLA Modules:
  0.0 330.6 jit_solution(7343783926037266920)
XLA Ops:
  7.9 0.8 stack_reshape.6
  8.6 0.8 stack_reshape.7
  9.6 0.7 convert_element_type.52
  10.3 1.1 copy-done.4
  11.4 0.7 copy-done.8
  12.1 0.7 copy-done.17
  12.7 17.6 %shard_map.339 = bf16[1088,1024]{1,0:T(8,128)(2,1)S(1)} custom-call(bf16[272,1024]{1,0:T(8,128)(2,1)S(1)} %copy-done.4, f32[1,1024]{1,0:T(1,128)S(1)} %bitcast.69, f32[1,1024]{1,0:T(1,128)S(1)} %bitcast.58), custom_call_target="tpu_custom_call" | custom-call | flops 24999999488 | bytes 2793472 | tf_op jit(solution)/shard_map/pallas_call | solution.py:569
  30.4 1.4 copy-done.19
  31.7 3.1 fusion.7.packed_ref
  34.9 12.5 %attend.1 = (bf16[1088,256]{1,0:T(8,128)(2,1)}, f32[1,2,1088,2]{3,2,1,0:T(8,128)}) custom-call(s32[1]{0:T(128)S(6)} %copy.53.lengths, bf16[1088,768]{1,0:T(8,128)(2,1)} %fusion.7.packed_ref), custom_call_target="tpu_custom_call" | custom-call | flops 2424307712 | bytes 2506752 | tf_op jit(solution)/shard_map/attend/pallas_call | solution.py:710
  47.5 1.0 copy-done
  48.6 31.6 %shard_map.340 = (bf16[1088,1024]{1,0:T(8,128)(2,1)S(1)}, f32[272,1024]{1,0:T(8,128)S(1)}, f32[272,1024]{1,0:T(8,128)S(1)}) custom-call(bf16[1088,256]{1,0:T(8,128)(2,1)S(1)} %copy-done, bf16[256,1024]{1,0:T(8,128)(2,1)S(1)} %copy-done.6, bf16[272,1024]{1,0:T(8,128)(2,1)S(1)} %copy-done.4, f32[1,1024]{1,0:T(1,128)S(1)} %bitcast.59, f32[1,1024]{1,0:T(1,128)S(1)} %bitcast.65, ...), custom_call_target="tpu_custom_call" | custom-call | flops 25570424832 | bytes 6115328 | tf_op jit(solution)/shard_map/pallas_call | solution.py:569
  80.2 6.2 %multiply_convert_fusion = (bf16[1088,1024]{1,0:T(8,128)(2,1)}, f32[1088,1024]{1,0:T(8,128)}) fusion(f32[1024]{0:T(1024)S(1)} %convert_element_type.52, bf16[1088,1024]{1,0:T(8,128)(2,1)S(1)} %get-tuple-element.42, bf16[1024,1024]{1,0:T(8,128)(2,1)S(1)} %copy-done.32), kind=kOutput, calls=%fused_computation.11 | convolution fusion | flops 2292842496 | bytes 11014144 | tf_op jit(solution)/shard_map/dot_general | solution.py:798
  86.5 35.8 %shard_map.341 = (bf16[1088,1024]{1,0:T(8,128)(2,1)}, bf16[272,1024]{1,0:T(8,128)(2,1)S(1)}, f32[3,8,1024]{2,1,0:T(8,128)S(1)}) custom-call(bf16[1088,1024]{1,0:T(8,128)(2,1)} %get-tuple-element.79.refs_0_, bf16[1024,1024]{1,0:T(8,128)(2,1)S(1)} %copy-done.2, f32[272,1024]{1,0:T(8,128)S(1)} %get-tuple-element.43.refs_2_.refs_3_, ...), custom_call_target="tpu_custom_call" | custom-call | flops 27281700864 | bytes 8892416 | tf_op jit(solution)/shard_map/pallas_call | solution.py:569
  122.3 5.9 %convolution_convert_fusion.2 = bf16[1024,1024]{1,0:T(8,128)(2,1)} fusion(bf16[1088,1024]{1,0:T(8,128)(2,1)S(1)} %copy-done.35, bf16[1088,1024]{1,0:T(8,128)(2,1)} %get-tuple-element.46), kind=kOutput, calls=%fused_computation.16 | convolution fusion | flops 2282749952 | bytes 6553600 | tf_op jit(solution)/shard_map/dot_general | solution.py:25
  128.3 7.8 %convert_reduce_fusion = (f32[1024]{0:T(1024)S(1)}, bf16[1088,1024]{1,0:T(8,128)(2,1)S(1)}) fusion(f32[1088,1024]{1,0:T(8,128)} %get-tuple-element.80, bf16[1088,1024]{1,0:T(8,128)(2,1)} %get-tuple-element.46, bf16[1024,1024]{1,0:T(8,128)(2,1)S(1)} %copy-done.2), kind=kOutput, calls=%fused_computation.10 | convolution fusion | flops 2306210816 | bytes 11014144 | tf_op jit(solution)/shard_map/dot_general | solution.py:19
  136.1 4.2 %convolution_convert_fusion.1.refs_7_ = bf16[1024,1024]{1,0:T(8,128)(2,1)} fusion(bf16[1088,1024]{1,0:T(8,128)(2,1)S(1)} %copy-done.21, bf16[1088,1024]{1,0:T(8,128)(2,1)S(1)} %get-tuple-element.66.refs_0_), kind=kOutput, calls=%fused_computation.15 | convolution fusion | flops 2282749952 | bytes 6553600 | tf_op jit(solution)/shard_map/dot_general | solution.py:25
  140.3 51.1 %shard_map.342 = (bf16[1088,1024]{1,0:T(8,128)(2,1)}, f32[272,1024]{1,0:T(8,128)S(1)}, bf16[128,1024]{1,0:T(8,128)(2,1)S(1)}, f32[5,8,1024]{2,1,0:T(8,128)S(1)}) custom-call(bf16[1088,1024]{1,0:T(8,128)(2,1)} %copy-done.34, bf16[1024,1024]{1,0:T(8,128)(2,1)} %refs_1_.6, f32[272,1024]{1,0:T(8,128)S(1)} %copy-done.25, f32[272,1024]{1,0:T(8,128)S(1)} %copy-done.27, ...), custom_call_target="tpu_custom_call" | custom-call | flops 27281700864 | bytes 12984320 | tf_op jit(solution)/shard_map/pallas_call | solution.py:569
  191.4 3.0 convolution_convert_fusion.4
  194.4 1.6 convolution_convert_fusion.grad_ref
  196.0 1.0 copy.42
  197.1 19.5 %attend_back.1 = (bf16[1088,768]{1,0:T(8,128)(2,1)}, f32[1,2,1,384]{3,2,1,0:T(1,128)}) custom-call(s32[1]{0:T(128)S(6)} %copy.53.lengths, bf16[1088,768]{1,0:T(8,128)(2,1)} %fusion.7.packed_ref, bf16[1088,256]{1,0:T(8,128)(2,1)} %convolution_convert_fusion.grad_ref, f32[1,2,2,1088]{3,2,1,0:T(2,128)} %bitcast.73), custom_call_target="tpu_custom_call" | custom-call | flops 6060769280 | bytes 4177920 | tf_op jit(solution)/shard_map/attend_back/pallas_call | solution.py:737
  216.5 5.6 %convolution_convert_fusion.3.refs_5_ = bf16[1024,768]{1,0:T(8,128)(2,1)} fusion(bf16[1088,1024]{1,0:T(8,128)(2,1)} %copy-done.19, bf16[1088,768]{1,0:T(8,128)(2,1)} %get-tuple-element.50.refs_0_), kind=kOutput, calls=%fused_computation.17 | convolution fusion | flops 1712062464 | bytes 5472256 | tf_op jit(solution)/shard_map/dot_general | solution.py:25
  222.5 1.2 copy-done.23
  223.8 86.1 %shard_map.343 = (f32[272,1024]{1,0:T(8,128)S(1)}, bf16[1024,768]{1,0:T(8,128)(2,1)S(1)}, bf16[1024,256]{1,0:T(8,128)(2,1)S(1)}, f32[10,1024]{1,0:T(8,128)S(1)},...) custom-call(bf16[1088,768]{1,0:T(8,128)(2,1)} %get-tuple-element.50.refs_0_, ...), custom_call_target="tpu_custom_call" | custom-call | flops 26711275520 | bytes 12967936 | tf_op jit(solution)/shard_map/pallas_call | solution.py:569
  310.6 1.1 copy.46
  311.7 1.9 convert_element_type.61
  313.6 0.6 copy-done.29
  314.2 2.5 convert_element_type.66
  317.9 4.1 %convert_element_type.67 = f32[1024,1024]{1,0:T(8,128)} convert(bf16[1024,1024]{1,0:T(8,128)(2,1)} %all-reduce.2.cloned.1.call-done) | non-fusion elementwise | flops 1048576 | bytes 6291456 | tf_op jit(solution)/shard_map/convert_element_type | solution.py:857
  322.0 0.8 copy.54
  322.8 1.0 copy.55
  (85 shorter events, 2.7 us)
Async XLA Ops:
  7.2 310.7 %all-reduce.2.cloned.1.call-start = ((), (), s32[]{:S(2)}) async-start(), calls=%async_computation | async-start | bytes 4194304 | tf_op jit(solution)/shard_map/psum | solution.py:806
  12.7 19.0 %copy-start.33 = (bf16[1024,768]{1,0:T(8,128)(2,1)S(1)}, bf16[1024,768]{1,0:T(8,128)(2,1)}, u32[]{:S(2)}) copy-start(bf16[1024,768]{1,0:T(8,128)(2,1)} %refs_1_.7) | copy-start | bytes 4718596
  30.4 1.4 copy-start.19
  34.9 12.6 %copy-start.6 = (bf16[256,1024]{1,0:T(8,128)(2,1)S(1)}, bf16[256,1024]{1,0:T(8,128)(2,1)}, u32[]{:S(2)}) copy-start(bf16[256,1024]{1,0:T(8,128)(2,1)} %refs_1_.4) | copy-start | bytes 1572868
  34.9 12.6 %copy-start.9 = (f32[1024]{0:T(1024)S(1)}, f32[1024]{0:T(1024)}, u32[]{:S(2)}) copy-start(f32[1024]{0:T(1024)} %param.28) | copy-start | bytes 12292
  34.9 12.6 %copy-start.10 = (f32[1024]{0:T(1024)S(1)}, f32[1024]{0:T(1024)}, u32[]{:S(2)}) copy-start(f32[1024]{0:T(1024)} %param.30) | copy-start | bytes 12292
  34.9 12.6 %copy-start.11 = (f32[1024]{0:T(1024)S(1)}, f32[1024]{0:T(1024)}, u32[]{:S(2)}) copy-start(f32[1024]{0:T(1024)} %param.32) | copy-start | bytes 12292
  34.9 12.6 %copy-start.15 = (f32[1024]{0:T(1024)S(1)}, f32[1024]{0:T(1024)}, u32[]{:S(2)}) copy-start(f32[1024]{0:T(1024)} %param.29) | copy-start | bytes 12292
  34.9 12.6 %copy-start.16 = (f32[1024]{0:T(1024)S(1)}, f32[1024]{0:T(1024)}, u32[]{:S(2)}) copy-start(f32[1024]{0:T(1024)} %param.31) | copy-start | bytes 12292
  48.5 31.6 %copy-start.32 = (bf16[1024,1024]{1,0:T(8,128)(2,1)S(1)}, bf16[1024,1024]{1,0:T(8,128)(2,1)}, u32[]{:S(2)}) copy-start(bf16[1024,1024]{1,0:T(8,128)(2,1)} %refs_1_.6) | copy-start | bytes 6291460
  80.1 6.3 %copy-start.20 = (bf16[1088,1024]{1,0:T(8,128)(2,1)}, bf16[1088,1024]{1,0:T(8,128)(2,1)S(1)}, u32[]{:S(2)}) copy-start(bf16[1088,1024]{1,0:T(8,128)(2,1)S(1)} %get-tuple-element.42) | copy-start | bytes 6684676
  80.2 6.3 %copy-start.24 = (f32[272,1024]{1,0:T(8,128)}, f32[272,1024]{1,0:T(8,128)S(1)}, u32[]{:S(2)}) copy-start(f32[272,1024]{1,0:T(8,128)S(1)} %get-tuple-element.47.refs_2_) | copy-start | bytes 3342340
  80.2 6.3 %copy-start.26 = (f32[272,1024]{1,0:T(8,128)}, f32[272,1024]{1,0:T(8,128)S(1)}, u32[]{:S(2)}) copy-start(f32[272,1024]{1,0:T(8,128)S(1)} %get-tuple-element.43.refs_2_.refs_3_) | copy-start | bytes 3342340
  80.2 6.3 %copy-start.2 = (bf16[1024,1024]{1,0:T(8,128)(2,1)S(1)}, bf16[1024,1024]{1,0:T(8,128)(2,1)}, u32[]{:S(2)}) copy-start(bf16[1024,1024]{1,0:T(8,128)(2,1)} %refs_1_.5) | copy-start | bytes 6291460
  80.2 6.3 %copy-start.3 = (bf16[272,1024]{1,0:T(8,128)(2,1)S(1)}, bf16[272,1024]{1,0:T(8,128)(2,1)}, u32[]{:S(2)}) copy-start(bf16[272,1024]{1,0:T(8,128)(2,1)} %refs_4_.1) | copy-start | bytes 1671172
  80.2 6.3 %copy-start.12 = (f32[1024]{0:T(1024)S(1)}, f32[1024]{0:T(1024)}, u32[]{:S(2)}) copy-start(f32[1024]{0:T(1024)} %param.36) | copy-start | bytes 12292
  80.2 6.3 %copy-start.13 = (f32[1024]{0:T(1024)S(1)}, f32[1024]{0:T(1024)}, u32[]{:S(2)}) copy-start(f32[1024]{0:T(1024)} %param.37) | copy-start | bytes 12292
  80.2 6.3 %copy-start.14 = (f32[1024]{0:T(1024)S(1)}, f32[1024]{0:T(1024)}, u32[]{:S(2)}) copy-start(f32[1024]{0:T(1024)} %param.38) | copy-start | bytes 12292
  86.5 35.8 %copy-start.35 = (bf16[1088,1024]{1,0:T(8,128)(2,1)S(1)}, bf16[1088,1024]{1,0:T(8,128)(2,1)}, u32[]{:S(2)}) copy-start(bf16[1088,1024]{1,0:T(8,128)(2,1)} %get-tuple-element.79.refs_0_) | copy-start | bytes 6684676
  128.3 7.8 %copy-start.21 = (bf16[1088,1024]{1,0:T(8,128)(2,1)S(1)}, bf16[1088,1024]{1,0:T(8,128)(2,1)}, u32[]{:S(2)}) copy-start(bf16[1088,1024]{1,0:T(8,128)(2,1)} %copy-done.20) | copy-start | bytes 6684676
  136.0 4.2 %copy-start.34 = (bf16[1088,1024]{1,0:T(8,128)(2,1)}, bf16[1088,1024]{1,0:T(8,128)(2,1)S(1)}, u32[]{:S(2)}) copy-start(bf16[1088,1024]{1,0:T(8,128)(2,1)S(1)} %get-tuple-element.66.refs_0_) | copy-start | bytes 6684676
  136.1 4.2 %copy-start.25 = (f32[272,1024]{1,0:T(8,128)S(1)}, f32[272,1024]{1,0:T(8,128)}, u32[]{:S(2)}) copy-start(f32[272,1024]{1,0:T(8,128)} %copy-done.24) | copy-start | bytes 3342340
  136.1 4.2 %copy-start.27 = (f32[272,1024]{1,0:T(8,128)S(1)}, f32[272,1024]{1,0:T(8,128)}, u32[]{:S(2)}) copy-start(f32[272,1024]{1,0:T(8,128)} %copy-done.26) | copy-start | bytes 3342340
  140.3 51.2 %copy-start.1 = (bf16[1088,256]{1,0:T(8,128)(2,1)S(1)}, bf16[1088,256]{1,0:T(8,128)(2,1)}, u32[]{:S(2)}) copy-start(bf16[1088,256]{1,0:T(8,128)(2,1)} %get-tuple-element.41.refs_0_) | copy-start | bytes 1671172
  191.4 4.6 %copy-start.22 = (f32[272,1024]{1,0:T(8,128)}, f32[272,1024]{1,0:T(8,128)S(1)}, u32[]{:S(2)}) copy-start(f32[272,1024]{1,0:T(8,128)S(1)} %get-tuple-element.51.refs_3_) | copy-start | bytes 3342340
  191.4 3.0 copy-start.7
  191.4 3.0 copy-start.28
  194.4 1.6 copy-start.30
  216.5 5.6 %copy-start.31 = (f32[1,2,1,384]{3,2,1,0:T(1,128)S(1)}, f32[1,2,1,384]{3,2,1,0:T(1,128)}, u32[]{:S(2)}) copy-start(f32[1,2,1,384]{3,2,1,0:T(1,128)} %get-tuple-element.54) | copy-start | bytes 9220
  216.5 6.0 %copy-start.5 = (bf16[272,1024]{1,0:T(8,128)(2,1)S(1)}, bf16[272,1024]{1,0:T(8,128)(2,1)}, u32[]{:S(2)}) copy-start(bf16[272,1024]{1,0:T(8,128)(2,1)} %refs_2_.3) | copy-start | bytes 1671172
  216.5 6.0 %copy-start.18 = (f32[1024]{0:T(1024)S(1)}, f32[1024]{0:T(1024)}, u32[]{:S(2)}) copy-start(f32[1024]{0:T(1024)} %param.22) | copy-start | bytes 12292
  311.7 2.5 copy-start.29
  (5 other events, 4.7 us)
Sparse Core Ops, SparseCore 0:
  128.4 115.8 all-reduce.1
